TPU v7x, 32 devices: a whole 2x2x4 slice. The times are simulated.
32 devices in a mesh: rep: 2 (over y), span: 2 (over core), seq: 4 (over z), tp: 2 (over x).
Axes of the slice: x: 2, y: 2, z: 4, core: 2. Of those that a mesh axis runs over, the one named last changes fastest.
Arguments:
- queries: bfloat16 [8, 512, 24, 128], P(('rep', 'span'), 'seq', 'tp'), parts along dimension 0, may hold values from -110 to 110
- key_states: bfloat16 [8, 512, 4, 128], P(('rep', 'span'), 'seq', 'tp'), parts along dimension 0, may hold values from -11 to 11
- value_states: bfloat16 [8, 512, 4, 128], P(('rep', 'span'), 'seq', 'tp'), parts along dimension 0, may hold values from -6 to 6
- out_weight: bfloat16 [3072, 6144], P('tp', 'seq'), may hold values from -0.109375 to 0.109375
- noise_table: float32 [64, 6144], P(None, 'tp'), may hold values from 0.5 to 2
- plan: int32 [8], P('rep'), parts along dimension 0, may hold values from 0 to 63
Outputs:
- branch_out: bfloat16 [8, 512, 6144], P(('rep', 'span'), 'seq', 'tp'), parts along dimension 0
There are 2 independent parts, one for each index of `rep`. A program takes and returns all parts, laid end to end along the dimension named above; an argument that names none is the same for every part. Nothing has to cross between parts.
All inputs are finite; a program needn't handle non-finite values.
Results may differ from a plain program's by a relative error of at most 0.014.
Values may be sent and summed in bfloat16 or wider, within the bound.
A program may use at most 128 MiB of HBM per device.

v0:
```python
import jax
import jax.numpy as jnp
from jax import lax
from jax.sharding import PartitionSpec as P


def fold_block(carried, query_rows, key_rows, value_rows, factor):
    maxima, totals, weighted = carried
    scores = (
        jnp.einsum("tkgd,skd->tkgs", query_rows, key_rows, preferred_element_type=jnp.float32)
        * factor
    )
    highest = jnp.maximum(maxima, jnp.max(scores, axis=-1))
    shrink = jnp.exp(maxima - highest)
    weights = jnp.exp(scores - highest[..., None])
    totals = totals * shrink + jnp.sum(weights, axis=-1)
    weighted = weighted * shrink[..., None] + jnp.einsum(
        "tkgs,skd->tkgd",
        weights.astype(jnp.bfloat16),
        value_rows,
        preferred_element_type=jnp.float32,
    )
    return (maxima * 0.0 + highest, totals, weighted)


def per_device(queries, key_states, value_states, out_weight, noise_table, plan):
    ch_dev, tok_dev, heads_local, head_size = queries.shape
    kv_local = key_states.shape[2]
    per_kv = heads_local // kv_local
    span_count = ch_dev * lax.axis_size("span")
    first_span = lax.axis_index("span") * ch_dev
    factor = head_size ** (-0.5)
    grouped = queries.reshape(ch_dev, tok_dev, kv_local, per_kv, head_size)
    start_max = jnp.full((ch_dev, tok_dev, kv_local, per_kv), -1e30, jnp.float32)
    start_tot = jnp.zeros((ch_dev, tok_dev, kv_local, per_kv), jnp.float32)
    start_acc = jnp.zeros((ch_dev, tok_dev, kv_local, per_kv, head_size), jnp.float32)
    span_rows = (
        lax.all_gather(key_states, "seq", axis=1, tiled=True),
        lax.all_gather(value_states, "seq", axis=1, tiled=True),
    )
    key_piece = lax.all_gather(span_rows[0], "span", axis=0, tiled=True)
    value_piece = lax.all_gather(span_rows[1], "span", axis=0, tiled=True)
    new_max = []
    new_tot = []
    new_acc = []
    for q_span in range(ch_dev):
        inner_state = (start_max[q_span], start_tot[q_span], start_acc[q_span])
        for k_span in range(span_count):

            def update(inner, q_span=q_span, k_span=k_span):
                return fold_block(
                    inner, grouped[q_span], key_piece[k_span], value_piece[k_span], factor
                )

            inner_state = lax.cond(
                k_span <= first_span + q_span, update, lambda inner: inner, inner_state
            )
        new_max.append(inner_state[0])
        new_tot.append(inner_state[1])
        new_acc.append(inner_state[2])
    attn = (
        (jnp.stack(new_acc) / jnp.stack(new_tot)[..., None])
        .reshape(ch_dev, tok_dev, heads_local * head_size)
        .astype(jnp.bfloat16)
    )
    columns = jnp.einsum(
        "ctf,fo->cto",
        lax.all_gather(attn, "seq", axis=1, tiled=True),
        out_weight,
        preferred_element_type=jnp.float32,
    )
    partial_out = lax.all_to_all(
        columns.astype(jnp.bfloat16), "seq", split_axis=1, concat_axis=2, tiled=True
    ).astype(columns.dtype)
    summed = lax.psum_scatter(
        partial_out.astype(jnp.bfloat16), "tp", scatter_dimension=2, tiled=True
    ).astype(jnp.float32)
    levels = lax.dynamic_slice_in_dim(plan, first_span, ch_dev)
    picks = (levels[:, None] == jnp.arange(noise_table.shape[0], dtype=jnp.int32)[None, :]).astype(
        jnp.float32
    )
    gates = jnp.dot(picks, noise_table, precision=lax.Precision.HIGHEST)
    return (summed * gates[:, None, :]).astype(jnp.bfloat16)


def solution(mesh):
    placed = (
        P(("rep", "span"), "seq", "tp", None),
        P(("rep", "span"), "seq", "tp", None),
        P(("rep", "span"), "seq", "tp", None),
        P("tp", "seq"),
        P(None, "tp"),
        P("rep"),
    )
    return jax.shard_map(
        per_device,
        mesh=mesh,
        in_specs=placed,
        out_specs=P(("rep", "span"), "seq", "tp"),
        check_vma=False,
    )
```

profile of v0, /device:TPU:0, one launch (start us, length us, event | category | flops | bytes accessed | tf_op | source)
XLA Modules:
  0.0 320.5 jit_solution(18199733619609409647)
XLA Ops:
  7.5 18.0 %all_gather.15 = bf16[2,512,2,128]{3,1,2,0:T(8,128)(2,1)} all-gather(bf16[2,128,2,128]{3,1,2,0:T(8,128)(2,1)S(1)} %copy.63), channel_id=1, replica_groups=mesh['rep'=2,'span'=2,'seq'=4,'tp'=2] {'seq'}, dimensions={1}, use_global_device_ids=true | all-gather | bytes 655360 | tf_op jit(solution)/shard_map/all_gather | solution.py:38
  26.5 17.0 %all_gather.17 = bf16[2,512,2,128]{3,1,2,0:T(8,128)(2,1)} all-gather(bf16[2,128,2,128]{3,1,2,0:T(8,128)(2,1)S(1)} %copy.64), channel_id=1, replica_groups=mesh['rep'=2,'span'=2,'seq'=4,'tp'=2] {'seq'}, dimensions={1}, use_global_device_ids=true | all-gather | bytes 655360 | tf_op jit(solution)/shard_map/all_gather | solution.py:39
  43.7 9.6 %all-gather.6.cloned.1.call-done = bf16[4,512,2,128]{3,1,2,0:T(8,128)(2,1)} async-done(((bf16[2,512,2,128]{3,1,2,0:T(8,128)(2,1)}), bf16[4,512,2,128]{3,1,2,0:T(8,128)(2,1)}) %all-gather.6.cloned.1.call-update) | async-done | bytes 1048592 | tf_op jit(solution)/shard_map/all_gather | solution.py:42
  53.3 6.1 %conditional.12 = (f32[128,2,6]{0,2,1:T(8,128)}, f32[128,2,6]{0,2,1:T(8,128)S(1)}, f32[128,2,6,128]{3,0,2,1:T(8,128)S(1)}) conditional(s32[]{:T(128)} %convert_element_type.70, () %tuple.93, (bf16[4,512,2,128]{3,1,2,0:T(8,128)(2,1)}, bf16[2,128,2,6,128]{4,1,3,2,0:T(8,128)(2,1)}, bf16[4,512,2,128]{3,1,2,0:T(8,128)(2,1)}) %tuple.190), branch_computations={%region_16.0_spmd, %region_17.0_spmd} | conditional | flops 409147392 | bytes 11210776 | solution.py:55
  53.3 1.7 bitcast_reduce_fusion.4
  57.5 1.9 fusion.93
  59.4 6.2 %conditional.13 = ((f32[128,2,6]{0,2,1:T(8,128)}, f32[128,2,6]{0,2,1:T(8,128)S(1)}, f32[128,2,6,128]{3,0,2,1:T(8,128)S(1)})) conditional(s32[]{:T(128)} %convert_element_type.69, (f32[128,2,6]{0,2,1:T(8,128)}, f32[128,2,6]{0,2,1:T(8,128)S(1)}, f32[128,2,6,128]{3,0,2,1:T(8,128)S(1)}) %conditional.12, (f32[128,2,6]{0,2,1:T(8,128)}, ...), branch_computations={%region_20.0_spmd, %region_21.0_spmd} | conditional | flops 409344000 | bytes 12032032 | solution.py:55
  59.4 1.7 bitcast_reduce_fusion.5
  63.6 2.0 fusion.115
  65.6 6.1 %conditional.8 = (f32[128,2,6]{0,2,1:T(8,128)}, f32[128,2,6]{0,2,1:T(8,128)S(1)}, f32[128,2,6,128]{3,0,2,1:T(8,128)S(1)}) conditional(s32[]{:T(128)} %convert_element_type.66, () %tuple.87, (bf16[4,512,2,128]{3,1,2,0:T(8,128)(2,1)}, bf16[2,128,2,6,128]{4,1,3,2,0:T(8,128)(2,1)}, bf16[4,512,2,128]{3,1,2,0:T(8,128)(2,1)}) %tuple.193), branch_computations={%region_0.0_spmd, %region_1.0_spmd} | conditional | flops 409147392 | bytes 11210776 | solution.py:55
  65.6 1.7 bitcast_reduce_fusion
  69.8 1.9 fusion.10
  72.0 1.5 conditional.15
  73.4 1.4 conditional.11
  75.0 1.6 copy.73
  76.6 2.9 fusion.171
  79.6 93.0 %all-gather.8.cloned.1.call-done = bf16[2,512,1536]{2,1,0:T(8,128)(2,1)} async-done(((bf16[2,128,1536]{2,1,0:T(8,128)(2,1)}), bf16[2,512,1536]{2,1,0:T(8,128)(2,1)}) %all-gather.8.cloned.1.call-update) | async-done | bytes 3145744 | tf_op jit(solution)/shard_map/all_gather | solution.py:68
  172.6 8.1 %fusion.168 = bf16[2,512,1536]{2,1,0:T(8,128)(2,1)S(1)} fusion(bf16[2,512,1536]{2,1,0:T(8,128)(2,1)} %all-gather.8.cloned.1.call-done, bf16[1536,1536]{1,0:T(8,128)(2,1)} %param.25), kind=kOutput, calls=%fused_computation.166 | convolution fusion | flops 4833411072 | bytes 11010048 | tf_op jit(solution)/shard_map/ctf,fo->cto/dot_general | solution.py:66
  180.7 3.2 %copy.74 = bf16[2,512,1536]{2,0,1:T(2,128)(2,1)S(1)} copy(bf16[2,512,1536]{2,1,0:T(8,128)(2,1)S(1)} %fusion.168) | data formatting | bytes 6291456 | tf_op jit(solution)/shard_map/convert_element_type | solution.py:73
  183.9 73.3 %all_to_all.18 = bf16[2,512,1536]{2,0,1:T(2,128)(2,1)S(1)} all-to-all(bf16[2,512,1536]{2,0,1:T(2,128)(2,1)S(1)} %copy.74), channel_id=1, replica_groups=mesh['rep'=2,'span'=2,'seq'=4,'tp'=2] {'seq'}, dimensions={1} | all-to-all | bytes 6291456 | tf_op jit(solution)/shard_map/all_to_all | solution.py:72
  257.2 4.1 %copy.75 = bf16[2,128,4,1536]{3,2,1,0:T(4,128)(2,1)} copy(bf16[2,128,4,1536]{3,0,1,2:T(2,128)(2,1)S(1)} %bitcast.326) | data formatting | bytes 6291456 | tf_op jit(solution)/shard_map/all_to_all | solution.py:72
  261.3 6.9 %all_to_all.16 = bf16[2,128,6144]{2,1,0:T(8,128)(2,1)} reshape(bf16[2,128,4,1536]{3,2,1,0:T(4,128)(2,1)} %copy.75) | data formatting | bytes 6291456 | tf_op jit(solution)/shard_map/all_to_all | solution.py:72
  269.4 41.7 %reduce-scatter.2.cloned.1.call-done = bf16[2,128,3072]{2,1,0:T(8,128)(2,1)} async-done(((bf16[2,128,6144]{2,1,0:T(8,128)(2,1)}), bf16[2,128,3072]{2,1,0:T(8,128)(2,1)}) %reduce-scatter.2.cloned.1.call-update) | async-done | bytes 1572880 | tf_op jit(solution)/shard_map/reduce_scatter | solution.py:75
  311.1 2.9 multiply_convert_fusion
  (36 shorter events, 14.0 us)
Async XLA Ops:
  6.5 262.4 %copy-start = (f32[64,3072]{1,0:T(8,128)S(1)}, f32[64,3072]{1,0:T(8,128)}, u32[]{:S(2)}) copy-start(f32[64,3072]{1,0:T(8,128)} %param.26) | copy-start | bytes 2359300
  6.5 37.2 %all-gather.4.cloned.1.call-start = ((), (), s32[]{:S(2)}) async-start(), calls=%async_computation.2 | async-start | bytes 1572864 | tf_op jit(solution)/shard_map/all_gather | solution.py:41
  25.6 27.7 %all-gather.6.cloned.1.call-start = ((), (), s32[]{:S(2)}) async-start(), calls=%async_computation.3 | async-start | bytes 1572864 | tf_op jit(solution)/shard_map/all_gather | solution.py:42
  43.6 129.0 %all-gather.8.cloned.1.call-start = ((), (), s32[]{:S(2)}) async-start(), calls=%async_computation.4 | async-start | bytes 3932160 | tf_op jit(solution)/shard_map/all_gather | solution.py:68
  79.6 231.5 %reduce-scatter.2.cloned.1.call-start = ((), (), s32[]{:S(2)}) async-start(), calls=%async_computation.5 | async-start | bytes 4718592 | tf_op jit(solution)/shard_map/reduce_scatter | solution.py:75
  268.3 0.7 copy-start.5
Sparse Core Ops, SparseCore 0:
  25.7 10.8 all-gather.3
  43.7 9.5 all-gather.5
  79.7 92.8 all-gather.7
  268.4 42.6 reduce-scatter.1
where the time goes:
time: 322 us; the launch traced here: 321 us
  waiting for transfers between devices  144 us (45%)
  blocking collectives  108 us (34%)
  local copies, waits for them, and re-layouts  22.1 us (7%)
  matrix products  19.2 us (6%)
  between operations  13.2 us (4%)
  other arithmetic  12.9 us (4%)
    all_gather x1, waiting for transfers between devices, per_device(): lax.all_gather(attn, 'seq', axis=1, tiled=True)  93 us
    all_to_all x1, blocking collectives, per_device(): lax.all_to_all(columns.astype(jnp.bfloat16), 'seq', split_axis=1, concat_...  73.3 us
    reduce_scatter x1, waiting for transfers between devices, per_device(): lax.psum_scatter(partial_out.astype(jnp.bfloat16), 'tp', scatter_dimensio...  41.7 us
    all_gather x1, blocking collectives, per_device(): lax.all_gather(key_states, 'seq', axis=1, tiled=True)  18 us
    all_gather x1, blocking collectives, per_device(): lax.all_gather(value_states, 'seq', axis=1, tiled=True)  17 us
    all_to_all x2, local copies, waits for them, and re-layouts, per_device(): lax.all_to_all(columns.astype(jnp.bfloat16), 'seq', split_axis=1, concat_...  11 us
    all_gather x1, waiting for transfers between devices, per_device(): value_piece = lax.all_gather(span_rows[1], 'span', axis=0, tiled=True)  9.6 us
    dot_general x1, matrix products, per_device(): jnp.einsum('ctf,fo->cto', lax.all_gather(attn, 'seq', axis=1, tiled=True)...  8.06 us
  transfers between devices with their start and end apart: 4, of which 3 were waited for; matrix products, arithmetic and copies ran while one was open for 0% of the time, Pallas kernels for 0%

commit v1 on v0

--- a/solution.py
+++ b/solution.py
@@ -69,8 +69,14 @@
         out_weight,
         preferred_element_type=jnp.float32,
     )
-    partial_out = lax.all_to_all(
-        columns.astype(jnp.bfloat16), "seq", split_axis=1, concat_axis=2, tiled=True
+    partial_out = jnp.concatenate(
+        lax.all_to_all(
+            jnp.stack(jnp.split(columns.astype(jnp.bfloat16), lax.axis_size("seq"), axis=1)),
+            "seq",
+            0,
+            0,
+        ),
+        axis=2,
     ).astype(columns.dtype)
     summed = lax.psum_scatter(
         partial_out.astype(jnp.bfloat16), "tp", scatter_dimension=2, tiled=True

time: 322 us -> 314 us (0.975)
  local copies, waits for them, and re-layouts: 22.1 us -> 14.3 us
    all_to_all x2 -> x0, local copies, waits for them, and re-layouts: 11 us -> none  [per_device(): lax.all_to_all(columns.astype(jnp.bfloat16), 'seq', split_axis=1, concat_...]
    reshape x0 -> x1, local copies, waits for them, and re-layouts: none -> 4.65 us  [per_device(): jnp.concatenate(lax.all_to_all(jnp.stack(jnp.split(columns.astype(jnp.bfl...]
where the time goes in v1:
time: 314 us; the launch traced here: 313 us
  waiting for transfers between devices  144 us (46%)
  blocking collectives  109 us (35%)
  matrix products  19.2 us (6%)
  local copies, waits for them, and re-layouts  14.3 us (5%)
  between operations  13.2 us (4%)
  other arithmetic  12.5 us (4%)
    all_gather x1, waiting for transfers between devices, per_device(): lax.all_gather(attn, 'seq', axis=1, tiled=True)  93 us
    all_to_all x1, blocking collectives, per_device(): lax.all_to_all(jnp.stack(jnp.split(columns.astype(jnp.bfloat16), lax.axis...  74.1 us
    reduce_scatter x1, waiting for transfers between devices, per_device(): lax.psum_scatter(partial_out.astype(jnp.bfloat16), 'tp', scatter_dimensio...  41.8 us
    all_gather x1, blocking collectives, per_device(): lax.all_gather(key_states, 'seq', axis=1, tiled=True)  18 us
    all_gather x1, blocking collectives, per_device(): lax.all_gather(value_states, 'seq', axis=1, tiled=True)  17 us
    all_gather x1, waiting for transfers between devices, per_device(): value_piece = lax.all_gather(span_rows[1], 'span', axis=0, tiled=True)  9.6 us
    dot_general x1, matrix products, per_device(): jnp.einsum('ctf,fo->cto', lax.all_gather(attn, 'seq', axis=1, tiled=True)...  8.05 us
  transfers between devices with their start and end apart: 4, of which 3 were waited for; matrix products, arithmetic and copies ran while one was open for 0% of the time, Pallas kernels for 0%

profile of v1, /device:TPU:0, one launch (start us, length us, event | category | flops | bytes accessed | tf_op | source)
XLA Modules:
  0.0 313.2 jit_solution(3246276837477421130)
XLA Ops:
  7.5 18.0 %all_gather.15 = bf16[2,512,2,128]{3,1,2,0:T(8,128)(2,1)} all-gather(bf16[2,128,2,128]{3,1,2,0:T(8,128)(2,1)S(1)} %copy.63), channel_id=1, replica_groups=mesh['rep'=2,'span'=2,'seq'=4,'tp'=2] {'seq'}, dimensions={1}, use_global_device_ids=true | all-gather | bytes 655360 | tf_op jit(solution)/shard_map/all_gather | solution.py:38
  26.5 17.0 %all_gather.17 = bf16[2,512,2,128]{3,1,2,0:T(8,128)(2,1)} all-gather(bf16[2,128,2,128]{3,1,2,0:T(8,128)(2,1)S(1)} %copy.64), channel_id=1, replica_groups=mesh['rep'=2,'span'=2,'seq'=4,'tp'=2] {'seq'}, dimensions={1}, use_global_device_ids=true | all-gather | bytes 655360 | tf_op jit(solution)/shard_map/all_gather | solution.py:39
  43.7 9.6 %all-gather.6.cloned.1.call-done = bf16[4,512,2,128]{3,1,2,0:T(8,128)(2,1)} async-done(((bf16[2,512,2,128]{3,1,2,0:T(8,128)(2,1)}), bf16[4,512,2,128]{3,1,2,0:T(8,128)(2,1)}) %all-gather.6.cloned.1.call-update) | async-done | bytes 1048592 | tf_op jit(solution)/shard_map/all_gather | solution.py:42
  53.3 6.1 %conditional.12 = (f32[128,2,6]{0,2,1:T(8,128)}, f32[128,2,6]{0,2,1:T(8,128)S(1)}, f32[128,2,6,128]{3,0,2,1:T(8,128)S(1)}) conditional(s32[]{:T(128)} %convert_element_type.70, () %tuple.93, (bf16[4,512,2,128]{3,1,2,0:T(8,128)(2,1)}, bf16[2,128,2,6,128]{4,1,3,2,0:T(8,128)(2,1)}, bf16[4,512,2,128]{3,1,2,0:T(8,128)(2,1)}) %tuple.193), branch_computations={%region_16.0_spmd, %region_17.0_spmd} | conditional | flops 409147392 | bytes 11210776 | solution.py:55
  53.3 1.7 bitcast_reduce_fusion.4
  55.6 1.2 fusion.85
  57.5 1.9 fusion.93
  59.4 6.2 %conditional.13 = ((f32[128,2,6]{0,2,1:T(8,128)}, f32[128,2,6]{0,2,1:T(8,128)S(1)}, f32[128,2,6,128]{3,0,2,1:T(8,128)S(1)})) conditional(s32[]{:T(128)} %convert_element_type.69, (f32[128,2,6]{0,2,1:T(8,128)}, f32[128,2,6]{0,2,1:T(8,128)S(1)}, f32[128,2,6,128]{3,0,2,1:T(8,128)S(1)}) %conditional.12, (f32[128,2,6]{0,2,1:T(8,128)}, ...), branch_computations={%region_20.0_spmd, %region_21.0_spmd} | conditional | flops 409344000 | bytes 12032032 | solution.py:55
  59.4 1.7 bitcast_reduce_fusion.5
  63.6 2.0 fusion.115
  65.6 6.1 %conditional.8 = (f32[128,2,6]{0,2,1:T(8,128)}, f32[128,2,6]{0,2,1:T(8,128)S(1)}, f32[128,2,6,128]{3,0,2,1:T(8,128)S(1)}) conditional(s32[]{:T(128)} %convert_element_type.66, () %tuple.87, (bf16[4,512,2,128]{3,1,2,0:T(8,128)(2,1)}, bf16[2,128,2,6,128]{4,1,3,2,0:T(8,128)(2,1)}, bf16[4,512,2,128]{3,1,2,0:T(8,128)(2,1)}) %tuple.196), branch_computations={%region_0.0_spmd, %region_1.0_spmd} | conditional | flops 409147392 | bytes 11210776 | solution.py:55
  65.6 1.7 bitcast_reduce_fusion
  69.8 1.9 fusion.10
  72.0 1.5 conditional.15
  73.4 1.4 conditional.11
  75.0 1.6 copy.73
  76.6 3.0 fusion.171
  79.6 93.0 %all-gather.8.cloned.1.call-done = bf16[2,512,1536]{2,1,0:T(8,128)(2,1)} async-done(((bf16[2,128,1536]{2,1,0:T(8,128)(2,1)}), bf16[2,512,1536]{2,1,0:T(8,128)(2,1)}) %all-gather.8.cloned.1.call-update) | async-done | bytes 3145744 | tf_op jit(solution)/shard_map/all_gather | solution.py:68
  172.6 8.1 %fusion.168 = bf16[2,512,1536]{2,1,0:T(8,128)(2,1)S(1)} fusion(bf16[2,512,1536]{2,1,0:T(8,128)(2,1)} %all-gather.8.cloned.1.call-done, bf16[1536,1536]{1,0:T(8,128)(2,1)} %param.25), kind=kOutput, calls=%fused_computation.166 | convolution fusion | flops 4833411072 | bytes 11010048 | tf_op jit(solution)/shard_map/ctf,fo->cto/dot_general | solution.py:66
  181.3 74.1 %all_to_all.5 = bf16[4,2,128,1536]{3,2,1,0:T(8,128)(2,1)} all-to-all(bf16[4,2,128,1536]{3,2,1,0:T(8,128)(2,1)S(1)} %pad_maximum_fusion), channel_id=1, replica_groups=mesh['rep'=2,'span'=2,'seq'=4,'tp'=2] {'seq'}, dimensions={0} | all-to-all | bytes 6291456 | tf_op jit(solution)/shard_map/all_to_all | solution.py:73
  255.4 4.7 %copy.74 = bf16[2,128,4,1536]{1,3,2,0:T(8,128)(2,1)} copy(bf16[2,128,4,1536]{3,1,0,2:T(8,128)(2,1)} %bitcast.334) | data formatting | bytes 6291456 | tf_op jit(solution)/shard_map/reshape | solution.py:72
  261.2 41.8 %reduce-scatter.2.cloned.1.call-done = bf16[2,128,3072]{1,2,0:T(8,128)(2,1)} async-done(((bf16[2,128,6144]{1,2,0:T(8,128)(2,1)}), bf16[2,128,3072]{1,2,0:T(8,128)(2,1)}) %reduce-scatter.2.cloned.1.call-update) | async-done | bytes 1572880 | tf_op jit(solution)/shard_map/reduce_scatter | solution.py:81
  303.0 2.1 multiply_convert_fusion
  305.1 1.6 copy.75
  (37 shorter events, 13.4 us)
Async XLA Ops:
  6.5 254.3 %copy-start = (f32[64,3072]{1,0:T(8,128)S(1)}, f32[64,3072]{1,0:T(8,128)}, u32[]{:S(2)}) copy-start(f32[64,3072]{1,0:T(8,128)} %param.26) | copy-start | bytes 2359300
  6.5 37.2 %all-gather.4.cloned.1.call-start = ((), (), s32[]{:S(2)}) async-start(), calls=%async_computation.2 | async-start | bytes 1572864 | tf_op jit(solution)/shard_map/all_gather | solution.py:41
  25.6 27.7 %all-gather.6.cloned.1.call-start = ((), (), s32[]{:S(2)}) async-start(), calls=%async_computation.3 | async-start | bytes 1572864 | tf_op jit(solution)/shard_map/all_gather | solution.py:42
  43.6 129.0 %all-gather.8.cloned.1.call-start = ((), (), s32[]{:S(2)}) async-start(), calls=%async_computation.4 | async-start | bytes 3932160 | tf_op jit(solution)/shard_map/all_gather | solution.py:68
  79.6 223.4 %reduce-scatter.2.cloned.1.call-start = ((), (), s32[]{:S(2)}) async-start(), calls=%async_computation.5 | async-start | bytes 4718592 | tf_op jit(solution)/shard_map/reduce_scatter | solution.py:81
  260.1 0.7 copy-start.5
Sparse Core Ops, SparseCore 0:
  25.7 10.8 all-gather.3
  43.7 9.5 all-gather.5
  79.7 92.8 all-gather.7
  260.3 42.6 reduce-scatter.1
